TPU v7x, 32 devices: a whole 2x2x4 slice. The times are simulated.
32 devices in a mesh: slab: 8 (over z, x), rhs: 4 (over y, core).
Axes of the slice: x: 2, y: 2, z: 4, core: 2. Of those that a mesh axis runs over, the one named last changes fastest.
Arguments:
- diag_blocks: float32 [8, 512, 512], P('slab'), may hold values from -1 to 2, as said below
- sub_blocks: float32 [8, 512, 512], P('slab'), may hold values from -1 to 1
- right_side: float32 [256, 4096], P('rhs', 'slab'), may hold values from -6 to 6
- boundary: float32 [512, 256], P(None, 'rhs'), may hold values from -6 to 6
Outputs:
- solution: float32 [256, 4096], P('rhs', 'slab')
Inputs may be any that keep to these rules, and one draw needn't show every extreme that they name: Each diag_blocks tile is lower triangular with diagonal entries from 0.8 to 1.25; each sub_blocks tile is upper triangular (zeros below its diagonal).
All inputs are finite; a program needn't handle non-finite values.
Results may differ from a plain program's by a relative error of at most 0.00021.
Values sent between devices are 32-bit elements; how exact they have to be, the bound alone decides.
A program may use at most 64 MiB of HBM per device.

v0:
```python
import jax
import jax.numpy as jnp
from jax import lax
from jax.sharding import PartitionSpec as P


def shifted(block, axis, distance):
    devices = range(lax.axis_size(axis))
    route = [(i - distance, i) for i in devices if i - distance in devices]
    return lax.ppermute(block, axis, route)


def matmul(left, right):
    return jnp.dot(left, right, precision=lax.Precision.HIGHEST)


def lower_solve(lower, right):
    return jax.scipy.linalg.solve_triangular(lower, right, lower=True)


def spike_stack(diag_blocks, first_cols):
    spikes = [lower_solve(diag_blocks[0], first_cols)]
    return jnp.stack(spikes)


def local(diag_blocks, sub_blocks, right_side, boundary):
    tile_count = diag_blocks.shape[0]
    width = diag_blocks.shape[1]
    columns = right_side.shape[0]
    tiles_rhs = right_side.reshape(columns, tile_count, width).transpose(1, 2, 0)
    partial_value = [lower_solve(diag_blocks[0], tiles_rhs[0])]
    spikes = spike_stack(diag_blocks, sub_blocks[0])
    last_spike = spikes[tile_count - 1]
    last_part = partial_value[tile_count - 1]
    is_first = lax.axis_index("slab") == 0

    def advance(step, carry):
        inflow_now, outflow = carry
        incoming = shifted(outflow, "slab", 1)
        inflow_new = jnp.where(is_first, boundary, incoming)
        return (inflow_new, last_part - matmul(last_spike, inflow_new))

    inflow, finished = lax.fori_loop(
        0, lax.axis_size("slab"), advance, (jnp.zeros_like(last_part), last_part)
    )
    solved = jnp.stack([partial_value[0] - matmul(spikes[0], inflow)])
    return solved.transpose(2, 0, 1).reshape(columns, tile_count * width)


def solution(mesh):
    in_specs = (P("slab", None, None), P("slab", None, None), P("rhs", "slab"), P(None, "rhs"))
    out_specs = P("rhs", "slab")
    return jax.shard_map(local, mesh=mesh, in_specs=in_specs, out_specs=out_specs, check_vma=False)
```

profile of v0, /device:TPU:24, one launch (start us, length us, event | category | flops | bytes accessed | tf_op | source)
XLA Modules:
  0.0 130.6 jit_solution(620049476975760827)
XLA Ops:
  0.0 1.3 %bitcast_select_fusion = f32[512,512]{1,0:T(8,128)S(1)} fusion(f32[1,512,512]{2,1,0:T(8,128)} %param.6), kind=kLoop, calls=%fused_computation.14 | loop fusion | flops 524288 | bytes 2097152 | tf_op jit(solution)/shard_map/jit(_solve_triangular)/triangular_solve | solution.py:18
  1.4 8.0 %while.14 = (s32[]{:T(128)}, f32[512,512]{1,0:T(8,128)S(1)}, s32[4,2]{0,1:T(2,128)S(1)}, f32[4,128,128]{2,1,0:T(8,128)S(1)}, s32[]{:T(128)}) while((s32[]{:T(128)}, f32[512,512]{1,0:T(8,128)S(1)}, s32[4,2]{0,1:T(2,128)S(1)}, f32[4,128,128]{2,1,0:T(8,128)S(1)}, s32[]{:T(128)}) %tuple.32), condition=%wide.while_cond, body=%wide.while_body.sunk | while | flops 2 | bytes 131189 | solution.py:18
  1.5 0.6 fusion.57
  2.1 1.3 %bitcast_dynamic-update-slice_fusion.2 = f32[4,128,128]{2,1,0:T(8,128)S(1)} fusion(f32[4,128,128]{2,1,0:T(8,128)S(1)} %get-tuple-element.152, s32[]{:T(128)S(6)} %copy.8, f32[512,512]{1,0:T(8,128)S(1)} %get-tuple-element.155, s32[]{:T(128)} %bitcast.80, s32[]{:T(128)} %bitcast.81), kind=kLoop, calls=%fused_computation.3.clone.1 | loop fusion | bytes 131084 | tf_op jit(solution)/shard_map/jit(_solve_triangular)/triangular_solve
  3.5 0.6 fusion.57
  4.1 1.3 %bitcast_dynamic-update-slice_fusion.2 = f32[4,128,128]{2,1,0:T(8,128)S(1)} fusion(f32[4,128,128]{2,1,0:T(8,128)S(1)} %get-tuple-element.152, s32[]{:T(128)S(6)} %copy.8, f32[512,512]{1,0:T(8,128)S(1)} %get-tuple-element.155, s32[]{:T(128)} %bitcast.80, s32[]{:T(128)} %bitcast.81), kind=kLoop, calls=%fused_computation.3.clone.1 | loop fusion | bytes 131084 | tf_op jit(solution)/shard_map/jit(_solve_triangular)/triangular_solve
  5.5 0.6 fusion.57
  6.1 1.3 %bitcast_dynamic-update-slice_fusion.2 = f32[4,128,128]{2,1,0:T(8,128)S(1)} fusion(f32[4,128,128]{2,1,0:T(8,128)S(1)} %get-tuple-element.152, s32[]{:T(128)S(6)} %copy.8, f32[512,512]{1,0:T(8,128)S(1)} %get-tuple-element.155, s32[]{:T(128)} %bitcast.80, s32[]{:T(128)} %bitcast.81), kind=kLoop, calls=%fused_computation.3.clone.1 | loop fusion | bytes 131084 | tf_op jit(solution)/shard_map/jit(_solve_triangular)/triangular_solve
  7.5 0.6 fusion.57
  8.1 1.3 %bitcast_dynamic-update-slice_fusion.2 = f32[4,128,128]{2,1,0:T(8,128)S(1)} fusion(f32[4,128,128]{2,1,0:T(8,128)S(1)} %get-tuple-element.152, s32[]{:T(128)S(6)} %copy.8, f32[512,512]{1,0:T(8,128)S(1)} %get-tuple-element.155, s32[]{:T(128)} %bitcast.80, s32[]{:T(128)} %bitcast.81), kind=kLoop, calls=%fused_computation.3.clone.1 | loop fusion | bytes 131084 | tf_op jit(solution)/shard_map/jit(_solve_triangular)/triangular_solve
  9.5 39.3 %custom-call.7 = f32[4,128,128]{1,2,0:T(8,128)S(1)} custom-call(f32[4,128,128]{2,1,0:T(8,128)S(1)} %get-tuple-element.49), custom_call_target="InvertDiagBlocksLowerTriangular" | custom-call | tf_op jit(solution)/shard_map/jit(_solve_triangular)/triangular_solve | solution.py:18
  49.0 0.2 convolution_subtract_fusion.6
  49.4 0.3 convolution_subtract_fusion.5
  49.9 0.4 convolution_subtract_fusion.4
  50.5 0.4 fusion.10
  50.9 0.4 convolution_subtract_fusion.1
  51.3 0.4 fusion.26
  51.8 0.4 convolution_subtract_fusion
  52.2 0.4 fusion.28
  52.6 0.6 convolution_subtract_fusion.2
  53.3 0.4 fusion.30
  53.8 0.8 copy-done
  54.6 73.3 %while.13 = (s32[]{:T(128)}, f32[512,64]{0,1:T(8,128)}, f32[512,64]{0,1:T(8,128)S(1)}, pred[]{:T(512)}, f32[512,64]{0,1:T(8,128)S(1)}, /*index=5*/f32[512,512]{1,0:T(8,128)S(1)}, f32[512,64]{0,1:T(8,128)S(1)}, s32[]{:T(128)}) while((s32[]{:T(128)}, f32[512,64]{0,1:T(8,128)}, f32[512,64]{0,1:T(8,128)S(1)}, pred[]{:T(512)}, ...), condition=%wide.region_1.2_spmd, body=%wide.region_0.1_spmd.sunk | while | flops 201392128 | bytes 2883738 | solution.py:43
  54.6 3.4 %collective-permute-start = (f32[512,64]{0,1:T(8,128)S(1)}, f32[512,64]{0,1:T(8,128)S(1)}, u32[]{:S(2)}, u32[]{:S(2)}) collective-permute-start(f32[512,64]{0,1:T(8,128)S(1)} %get-tuple-element.169), channel_id=1, source_target_pairs={{0,4},{4,8},{8,12},{12,16},{16,20},{20,24},{24,28},{1,5},{5,9},{9,... | collective-permute-start | bytes 393224 | tf_op jit(solution)/shard_map/while/body/eval_jaxpr/ppermute | solution.py:10
  58.0 4.6 %collective-permute-done = f32[512,64]{0,1:T(8,128)S(1)} collective-permute-done((f32[512,64]{0,1:T(8,128)S(1)}, f32[512,64]{0,1:T(8,128)S(1)}, u32[]{:S(2)}, u32[]{:S(2)}) %collective-permute-start) | collective-permute-done | bytes 131104 | tf_op jit(solution)/shard_map/while/body/eval_jaxpr/ppermute | solution.py:10
  62.6 1.1 fusion.56
  63.8 2.5 %collective-permute-start = (f32[512,64]{0,1:T(8,128)S(1)}, f32[512,64]{0,1:T(8,128)S(1)}, u32[]{:S(2)}, u32[]{:S(2)}) collective-permute-start(f32[512,64]{0,1:T(8,128)S(1)} %get-tuple-element.169), channel_id=1, source_target_pairs={{0,4},{4,8},{8,12},{12,16},{16,20},{20,24},{24,28},{1,5},{5,9},{9,... | collective-permute-start | bytes 393224 | tf_op jit(solution)/shard_map/while/body/eval_jaxpr/ppermute | solution.py:10
  66.3 5.2 %collective-permute-done = f32[512,64]{0,1:T(8,128)S(1)} collective-permute-done((f32[512,64]{0,1:T(8,128)S(1)}, f32[512,64]{0,1:T(8,128)S(1)}, u32[]{:S(2)}, u32[]{:S(2)}) %collective-permute-start) | collective-permute-done | bytes 131104 | tf_op jit(solution)/shard_map/while/body/eval_jaxpr/ppermute | solution.py:10
  71.6 1.1 fusion.56
  72.7 1.9 %collective-permute-start = (f32[512,64]{0,1:T(8,128)S(1)}, f32[512,64]{0,1:T(8,128)S(1)}, u32[]{:S(2)}, u32[]{:S(2)}) collective-permute-start(f32[512,64]{0,1:T(8,128)S(1)} %get-tuple-element.169), channel_id=1, source_target_pairs={{0,4},{4,8},{8,12},{12,16},{16,20},{20,24},{24,28},{1,5},{5,9},{9,... | collective-permute-start | bytes 393224 | tf_op jit(solution)/shard_map/while/body/eval_jaxpr/ppermute | solution.py:10
  74.6 5.8 %collective-permute-done = f32[512,64]{0,1:T(8,128)S(1)} collective-permute-done((f32[512,64]{0,1:T(8,128)S(1)}, f32[512,64]{0,1:T(8,128)S(1)}, u32[]{:S(2)}, u32[]{:S(2)}) %collective-permute-start) | collective-permute-done | bytes 131104 | tf_op jit(solution)/shard_map/while/body/eval_jaxpr/ppermute | solution.py:10
  80.5 1.1 fusion.56
  81.6 1.9 %collective-permute-start = (f32[512,64]{0,1:T(8,128)S(1)}, f32[512,64]{0,1:T(8,128)S(1)}, u32[]{:S(2)}, u32[]{:S(2)}) collective-permute-start(f32[512,64]{0,1:T(8,128)S(1)} %get-tuple-element.169), channel_id=1, source_target_pairs={{0,4},{4,8},{8,12},{12,16},{16,20},{20,24},{24,28},{1,5},{5,9},{9,... | collective-permute-start | bytes 393224 | tf_op jit(solution)/shard_map/while/body/eval_jaxpr/ppermute | solution.py:10
  83.6 5.8 %collective-permute-done = f32[512,64]{0,1:T(8,128)S(1)} collective-permute-done((f32[512,64]{0,1:T(8,128)S(1)}, f32[512,64]{0,1:T(8,128)S(1)}, u32[]{:S(2)}, u32[]{:S(2)}) %collective-permute-start) | collective-permute-done | bytes 131104 | tf_op jit(solution)/shard_map/while/body/eval_jaxpr/ppermute | solution.py:10
  89.4 1.1 fusion.56
  90.6 1.9 %collective-permute-start = (f32[512,64]{0,1:T(8,128)S(1)}, f32[512,64]{0,1:T(8,128)S(1)}, u32[]{:S(2)}, u32[]{:S(2)}) collective-permute-start(f32[512,64]{0,1:T(8,128)S(1)} %get-tuple-element.169), channel_id=1, source_target_pairs={{0,4},{4,8},{8,12},{12,16},{16,20},{20,24},{24,28},{1,5},{5,9},{9,... | collective-permute-start | bytes 393224 | tf_op jit(solution)/shard_map/while/body/eval_jaxpr/ppermute | solution.py:10
  92.5 5.8 %collective-permute-done = f32[512,64]{0,1:T(8,128)S(1)} collective-permute-done((f32[512,64]{0,1:T(8,128)S(1)}, f32[512,64]{0,1:T(8,128)S(1)}, u32[]{:S(2)}, u32[]{:S(2)}) %collective-permute-start) | collective-permute-done | bytes 131104 | tf_op jit(solution)/shard_map/while/body/eval_jaxpr/ppermute | solution.py:10
  98.4 1.1 fusion.56
  99.5 1.9 %collective-permute-start = (f32[512,64]{0,1:T(8,128)S(1)}, f32[512,64]{0,1:T(8,128)S(1)}, u32[]{:S(2)}, u32[]{:S(2)}) collective-permute-start(f32[512,64]{0,1:T(8,128)S(1)} %get-tuple-element.169), channel_id=1, source_target_pairs={{0,4},{4,8},{8,12},{12,16},{16,20},{20,24},{24,28},{1,5},{5,9},{9,... | collective-permute-start | bytes 393224 | tf_op jit(solution)/shard_map/while/body/eval_jaxpr/ppermute | solution.py:10
  101.4 6.1 %collective-permute-done = f32[512,64]{0,1:T(8,128)S(1)} collective-permute-done((f32[512,64]{0,1:T(8,128)S(1)}, f32[512,64]{0,1:T(8,128)S(1)}, u32[]{:S(2)}, u32[]{:S(2)}) %collective-permute-start) | collective-permute-done | bytes 131104 | tf_op jit(solution)/shard_map/while/body/eval_jaxpr/ppermute | solution.py:10
  107.5 1.1 fusion.56
  108.7 1.9 %collective-permute-start = (f32[512,64]{0,1:T(8,128)S(1)}, f32[512,64]{0,1:T(8,128)S(1)}, u32[]{:S(2)}, u32[]{:S(2)}) collective-permute-start(f32[512,64]{0,1:T(8,128)S(1)} %get-tuple-element.169), channel_id=1, source_target_pairs={{0,4},{4,8},{8,12},{12,16},{16,20},{20,24},{24,28},{1,5},{5,9},{9,... | collective-permute-start | bytes 393224 | tf_op jit(solution)/shard_map/while/body/eval_jaxpr/ppermute | solution.py:10
  110.6 7.2 %collective-permute-done = f32[512,64]{0,1:T(8,128)S(1)} collective-permute-done((f32[512,64]{0,1:T(8,128)S(1)}, f32[512,64]{0,1:T(8,128)S(1)}, u32[]{:S(2)}, u32[]{:S(2)}) %collective-permute-start) | collective-permute-done | bytes 131104 | tf_op jit(solution)/shard_map/while/body/eval_jaxpr/ppermute | solution.py:10
  117.8 1.1 fusion.56
  119.0 1.9 %collective-permute-start = (f32[512,64]{0,1:T(8,128)S(1)}, f32[512,64]{0,1:T(8,128)S(1)}, u32[]{:S(2)}, u32[]{:S(2)}) collective-permute-start(f32[512,64]{0,1:T(8,128)S(1)} %get-tuple-element.169), channel_id=1, source_target_pairs={{0,4},{4,8},{8,12},{12,16},{16,20},{20,24},{24,28},{1,5},{5,9},{9,... | collective-permute-start | bytes 393224 | tf_op jit(solution)/shard_map/while/body/eval_jaxpr/ppermute | solution.py:10
  120.9 5.8 %collective-permute-done = f32[512,64]{0,1:T(8,128)S(1)} collective-permute-done((f32[512,64]{0,1:T(8,128)S(1)}, f32[512,64]{0,1:T(8,128)S(1)}, u32[]{:S(2)}, u32[]{:S(2)}) %collective-permute-start) | collective-permute-done | bytes 131104 | tf_op jit(solution)/shard_map/while/body/eval_jaxpr/ppermute | solution.py:10
  126.8 1.1 fusion.56
  127.9 2.7 %fusion.1 = f32[64,512]{1,0:T(8,128)} fusion(f32[512,64]{0,1:T(8,128)} %get-tuple-element.41, f32[128,64]{0,1:T(8,128)S(1)} %fusion.31, f32[128,64]{0,1:T(8,128)S(1)} %fusion.29, f32[128,64]{0,1:T(8,128)S(1)} %fusion.27, f32[128,64]{0,1:T(8,128)S(1)} %fusion.25, f32[128,512]{1,0:T(8,128)S(1)} %fusion.30, f32[128,512]{1,0:T(8,128)S(1)} %fusion.28, ...), kind=kOutput, calls=%fused_computation.9 | convolution fusion | flops 202244096 | bytes 1441792 | tf_op jit(solution)/shard_map/dot_general | solution.py:14
  (44 shorter events, 1.3 us)
Async XLA Ops:
  1.4 47.4 %copy-start.3 = (f32[64,512]{1,0:T(8,128)S(1)}, f32[64,512]{1,0:T(8,128)}, u32[]{:S(2)}) copy-start(f32[64,512]{1,0:T(8,128)} %param.8) | copy-start | bytes 393220
  9.4 41.1 %copy-start.2 = (f32[1,512,512]{2,1,0:T(8,128)S(1)}, f32[1,512,512]{2,1,0:T(8,128)}, u32[]{:S(2)}) copy-start(f32[1,512,512]{2,1,0:T(8,128)} %param.7) | copy-start | bytes 3145732
  53.7 0.9 copy-start
  54.6 8.0 %collective-permute-start = (f32[512,64]{0,1:T(8,128)S(1)}, f32[512,64]{0,1:T(8,128)S(1)}, u32[]{:S(2)}, u32[]{:S(2)}) collective-permute-start(f32[512,64]{0,1:T(8,128)S(1)} %get-tuple-element.169), channel_id=1, source_target_pairs={{0,4},{4,8},{8,12},{12,16},{16,20},{20,24},{24,28},{1,5},{5,9},{9,... | collective-permute-start | bytes 393224 | tf_op jit(solution)/shard_map/while/body/eval_jaxpr/ppermute | solution.py:10
  62.6 1.1 copy-start.1
  63.8 7.8 %collective-permute-start = (f32[512,64]{0,1:T(8,128)S(1)}, f32[512,64]{0,1:T(8,128)S(1)}, u32[]{:S(2)}, u32[]{:S(2)}) collective-permute-start(f32[512,64]{0,1:T(8,128)S(1)} %get-tuple-element.169), channel_id=1, source_target_pairs={{0,4},{4,8},{8,12},{12,16},{16,20},{20,24},{24,28},{1,5},{5,9},{9,... | collective-permute-start | bytes 393224 | tf_op jit(solution)/shard_map/while/body/eval_jaxpr/ppermute | solution.py:10
  71.6 1.1 copy-start.1
  72.7 7.8 %collective-permute-start = (f32[512,64]{0,1:T(8,128)S(1)}, f32[512,64]{0,1:T(8,128)S(1)}, u32[]{:S(2)}, u32[]{:S(2)}) collective-permute-start(f32[512,64]{0,1:T(8,128)S(1)} %get-tuple-element.169), channel_id=1, source_target_pairs={{0,4},{4,8},{8,12},{12,16},{16,20},{20,24},{24,28},{1,5},{5,9},{9,... | collective-permute-start | bytes 393224 | tf_op jit(solution)/shard_map/while/body/eval_jaxpr/ppermute | solution.py:10
  80.5 1.1 copy-start.1
  81.6 7.8 %collective-permute-start = (f32[512,64]{0,1:T(8,128)S(1)}, f32[512,64]{0,1:T(8,128)S(1)}, u32[]{:S(2)}, u32[]{:S(2)}) collective-permute-start(f32[512,64]{0,1:T(8,128)S(1)} %get-tuple-element.169), channel_id=1, source_target_pairs={{0,4},{4,8},{8,12},{12,16},{16,20},{20,24},{24,28},{1,5},{5,9},{9,... | collective-permute-start | bytes 393224 | tf_op jit(solution)/shard_map/while/body/eval_jaxpr/ppermute | solution.py:10
  89.4 1.1 copy-start.1
  90.6 7.8 %collective-permute-start = (f32[512,64]{0,1:T(8,128)S(1)}, f32[512,64]{0,1:T(8,128)S(1)}, u32[]{:S(2)}, u32[]{:S(2)}) collective-permute-start(f32[512,64]{0,1:T(8,128)S(1)} %get-tuple-element.169), channel_id=1, source_target_pairs={{0,4},{4,8},{8,12},{12,16},{16,20},{20,24},{24,28},{1,5},{5,9},{9,... | collective-permute-start | bytes 393224 | tf_op jit(solution)/shard_map/while/body/eval_jaxpr/ppermute | solution.py:10
  98.4 1.1 copy-start.1
  99.5 8.0 %collective-permute-start = (f32[512,64]{0,1:T(8,128)S(1)}, f32[512,64]{0,1:T(8,128)S(1)}, u32[]{:S(2)}, u32[]{:S(2)}) collective-permute-start(f32[512,64]{0,1:T(8,128)S(1)} %get-tuple-element.169), channel_id=1, source_target_pairs={{0,4},{4,8},{8,12},{12,16},{16,20},{20,24},{24,28},{1,5},{5,9},{9,... | collective-permute-start | bytes 393224 | tf_op jit(solution)/shard_map/while/body/eval_jaxpr/ppermute | solution.py:10
  107.5 1.1 copy-start.1
  108.7 9.1 %collective-permute-start = (f32[512,64]{0,1:T(8,128)S(1)}, f32[512,64]{0,1:T(8,128)S(1)}, u32[]{:S(2)}, u32[]{:S(2)}) collective-permute-start(f32[512,64]{0,1:T(8,128)S(1)} %get-tuple-element.169), channel_id=1, source_target_pairs={{0,4},{4,8},{8,12},{12,16},{16,20},{20,24},{24,28},{1,5},{5,9},{9,... | collective-permute-start | bytes 393224 | tf_op jit(solution)/shard_map/while/body/eval_jaxpr/ppermute | solution.py:10
  117.8 1.1 copy-start.1
  119.0 7.8 %collective-permute-start = (f32[512,64]{0,1:T(8,128)S(1)}, f32[512,64]{0,1:T(8,128)S(1)}, u32[]{:S(2)}, u32[]{:S(2)}) collective-permute-start(f32[512,64]{0,1:T(8,128)S(1)} %get-tuple-element.169), channel_id=1, source_target_pairs={{0,4},{4,8},{8,12},{12,16},{16,20},{20,24},{24,28},{1,5},{5,9},{9,... | collective-permute-start | bytes 393224 | tf_op jit(solution)/shard_map/while/body/eval_jaxpr/ppermute | solution.py:10
  126.7 1.1 copy-start.1
where the time goes:
time: 131 us
  waiting for transfers between devices  46.4 us (35%)
  other arithmetic  40.9 us (31%)
  starting transfers between devices  17.4 us (13%)
  matrix products  16.4 us (13%)
  local copies, waits for them, and re-layouts  8.84 us (7%)
    ppermute x8, waiting for transfers between devices, shifted(): return lax.ppermute(block, axis, route)  46.4 us
    another operation x5, other arithmetic, lower_solve(): return jax.scipy.linalg.solve_triangular(lower, right, lower=True)  40.7 us
    ppermute x8, starting transfers between devices, shifted(): return lax.ppermute(block, axis, route)  17.4 us
    dot_general x9, matrix products, matmul(): return jnp.dot(left, right, precision=lax.Precision.HIGHEST)  11.7 us
    another operation x12, local copies, waits for them, and re-layouts  7.96 us
    another operation x14, matrix products, lower_solve(): return jax.scipy.linalg.solve_triangular(lower, right, lower=True)  4.75 us
  transfers between devices with their start and end apart: 8, of which 8 were waited for; matrix products, arithmetic and copies ran while one was open for 0% of the time, Pallas kernels for 0%

commit v1 on v0

v1 whole, which is shorter than its diff:
```python
import functools

import jax
import jax.numpy as jnp
from jax import lax
from jax.experimental import pallas as pl
from jax.experimental.pallas import tpu as pltpu
from jax.sharding import PartitionSpec as P

BASE = 128
CHUNKS = 4
MESH = pl.DeviceIdType.MESH
NN = (((1,), (0,)), ((), ()))
NT = (((1,), (1,)), ((), ()))


def split(value):
    high = value.astype(jnp.bfloat16)
    low = (value - high.astype(jnp.float32)).astype(jnp.bfloat16)
    return high, low


def mul(left, right, dims=NN):
    dot = functools.partial(lax.dot_general, dimension_numbers=dims, preferred_element_type=jnp.float32)
    return dot(left[0], right[0]) + (dot(left[0], right[1]) + dot(left[1], right[0]))


def kernel(n, diag_hbm, sub_hbm, right_hbm, bound_hbm, out_hbm,
           diag, sub, right, inverse, norm, inv_hi, inv_lo, subt_hi, subt_lo,
           spike_hi, spike_lo, part, inflow, solved,
           load_sem, send_sem, recv_sem, store_sem):
    me = lax.axis_index("slab")
    width = diag.shape[0]
    columns = right.shape[0]
    rows = columns // CHUNKS
    loads = []
    for k, (src, dst) in enumerate(((diag_hbm.at[0], diag), (sub_hbm.at[0], sub), (right_hbm, right))):
        loads.append(pltpu.make_async_copy(src, dst, load_sem.at[k]))
        loads[-1].start()
    first, last = me == 0, me == n - 1
    seed = pltpu.make_async_copy(bound_hbm, inflow, load_sem.at[3])

    @pl.when(first)
    def _():
        seed.start()

    after, before = lax.rem(me + 1, n), lax.rem(me + n - 1, n)
    barrier = pltpu.get_barrier_semaphore()
    for other in (before, after):
        pl.semaphore_signal(barrier, inc=1, device_id={"slab": other}, device_id_type=MESH)

    row = lax.broadcasted_iota(jnp.int32, (BASE, BASE), 0)
    col = lax.broadcasted_iota(jnp.int32, (BASE, BASE), 1)
    apart = jnp.where(row > col, row ^ col, 0)
    eye = jnp.where(row == col, 1.0, 0.0).astype(jnp.float32)
    loads[0].wait()
    starts = range(0, width, BASE)
    blocks, scales = [], []
    for at in starts:
        tile = diag[at:at + BASE, at:at + BASE]
        only = tile * eye
        scale = 1.0 / jnp.sum(only, axis=1, keepdims=True)
        scales.append(1.0 / jnp.sum(only, axis=0, keepdims=True))
        for left in range(0, at, BASE):
            norm[at:at + BASE, left:left + BASE] = diag[at:at + BASE, left:left + BASE] * scale
        blocks.append(tile * scale)
    found = [eye - jnp.where(apart == 1, block, 0.0) for block in blocks]
    size = 2
    while size < BASE:
        level = (apart >= size) & (apart < 2 * size)
        pairs = [split(x) for x in found]
        lower = [split(jnp.where(level, block, 0.0)) for block in blocks]
        half = [mul(a, b) for a, b in zip(lower, pairs)]
        found = [x - mul(pair, split(h)) for x, pair, h in zip(found, pairs, half)]
        size *= 2
    for at, x in zip(starts, found):
        inverse[at:at + BASE, at:at + BASE] = x
        for over in range(at + BASE, width, BASE):
            inverse[at:at + BASE, over:over + BASE] = jnp.zeros((BASE, BASE), jnp.float32)
    while size < width:
        for at in range(0, width, 2 * size):
            mid, end = at + size, at + 2 * size
            half = mul(split(norm[mid:end, at:mid]), split(inverse[at:mid, at:mid]))
            inverse[mid:end, at:mid] = -mul(split(inverse[mid:end, mid:end]), split(half))
        size *= 2
    for at, scale in zip(starts, scales):
        high, low = split(inverse[:, at:at + BASE] * scale)
        inv_hi[:, at:at + BASE] = high
        inv_lo[:, at:at + BASE] = low

    loads[1].wait()
    high, low = split(sub[...].T)
    subt_hi[...] = high
    subt_lo[...] = low
    cut = width // 2

    def take(pair, rows_at, cols_at):
        return pair[0][rows_at, cols_at], pair[1][rows_at, cols_at]

    subt, inv, spike = (subt_hi, subt_lo), (inv_hi, inv_lo), (spike_hi, spike_lo)
    top, bot, full = slice(0, cut), slice(cut, width), slice(0, width)

    def put(rows_at, cols_at, value):
        high, low = split(value)
        spike_hi[rows_at, cols_at] = high
        spike_lo[rows_at, cols_at] = low

    put(full, top, mul(take(subt, full, top), take(inv, top, top), NT))
    put(top, bot, mul(take(subt, top, top), take(inv, bot, top), NT))
    put(bot, bot, mul(take(subt, bot, full), take(inv, bot, full), NT))
    loads[2].wait()
    given = split(right[...])
    part[:, top] = mul((given[0][:, top], given[1][:, top]), take(inv, top, top), NT)
    part[:, bot] = mul(given, take(inv, bot, full), NT)


    def send(c):
        at = slice(c * rows, (c + 1) * rows)
        return pltpu.make_async_remote_copy(
            src_ref=solved.at[at], dst_ref=inflow.at[at], send_sem=send_sem.at[c], recv_sem=recv_sem.at[c],
            device_id={"slab": after}, device_id_type=MESH)

    def store(c):
        at = slice(c * rows, (c + 1) * rows)
        return pltpu.make_async_copy(solved.at[at], out_hbm.at[at], store_sem.at[c])

    @pl.when(first)
    def _():
        seed.wait()

    pl.semaphore_wait(barrier, 2)
    for c in range(CHUNKS):
        at = slice(c * rows, (c + 1) * rows)

        @pl.when(jnp.logical_not(first))
        def _():
            send(c).wait_recv()

        high, low = split(inflow[at, :])
        dot = functools.partial(jnp.dot, preferred_element_type=jnp.float32)
        both = dot(jnp.concatenate([high, low], axis=0), spike_hi[...])
        solved[at, :] = part[at, :] - (both[:rows] + both[rows:] + dot(high, spike_lo[...]))

        @pl.when(jnp.logical_not(last))
        def _():
            send(c).start()

        store(c).start()
    for c in range(CHUNKS):
        store(c).wait()

        @pl.when(jnp.logical_not(last))
        def _():
            send(c).wait_send()


def solution(mesh):
    n = mesh.shape["slab"]

    def local(diag_blocks, sub_blocks, right_side, boundary):
        width = diag_blocks.shape[1]
        columns = right_side.shape[0]
        square, flat = (width, width), (columns, width)
        f32, bf16 = jnp.float32, jnp.bfloat16
        return pl.pallas_call(
            functools.partial(kernel, n),
            out_shape=jax.ShapeDtypeStruct(right_side.shape, f32),
            in_specs=[pl.BlockSpec(memory_space=pl.ANY)] * 4,
            out_specs=pl.BlockSpec(memory_space=pl.ANY),
            scratch_shapes=[
                pltpu.VMEM(square, f32), pltpu.VMEM(square, f32), pltpu.VMEM(flat, f32),
                pltpu.VMEM(square, f32), pltpu.VMEM(square, f32), pltpu.VMEM(square, bf16), pltpu.VMEM(square, bf16),
                pltpu.VMEM(square, bf16), pltpu.VMEM(square, bf16), pltpu.VMEM(square, bf16), pltpu.VMEM(square, bf16),
                pltpu.VMEM(flat, f32), pltpu.VMEM(flat, f32), pltpu.VMEM(flat, f32),
                pltpu.SemaphoreType.DMA((4,)), pltpu.SemaphoreType.DMA((CHUNKS,)),
                pltpu.SemaphoreType.DMA((CHUNKS,)), pltpu.SemaphoreType.DMA((CHUNKS,)),
            ],
            compiler_params=pltpu.CompilerParams(collective_id=0, has_side_effects=True),
        )(diag_blocks, sub_blocks, right_side, boundary.T)

    in_specs = (P("slab", None, None), P("slab", None, None), P("rhs", "slab"), P(None, "rhs"))
    return jax.shard_map(local, mesh=mesh, in_specs=in_specs, out_specs=P("rhs", "slab"), check_vma=False)
```

time: 131 us -> 32.9 us (0.25)
  the two profiles are of different devices: /device:TPU:24 before, /device:TPU:30 now
where the time goes in v1:
time: 32.9 us; the launch traced here: 32.7 us
  Pallas kernels  31.2 us (95%)
  local copies, waits for them, and re-layouts  1.57 us (5%)
    pallas_call x1, Pallas kernels, local(): pl.pallas_call(functools.partial(kernel, n), out_shape=jax.ShapeDtypeStru...  31.2 us
    unnamed x1, local copies, waits for them, and re-layouts  1.57 us

profile of v1, /device:TPU:30, one launch (start us, length us, event | category | flops | bytes accessed | tf_op | source)
XLA Modules:
  0.0 32.7 jit_solution(13916088203811193760)
XLA Ops:
  0.0 31.2 %shard_map.46 = f32[64,512]{1,0:T(8,128)} custom-call(f32[1,512,512]{2,1,0:T(8,128)} %diag_hbm.1, f32[1,512,512]{2,1,0:T(8,128)} %sub_hbm.1, f32[64,512]{1,0:T(8,128)} %right_hbm.1, f32[64,512]{1,0:T(8,128)} %bitcast.1), custom_call_target="tpu_custom_call" | custom-call | tf_op jit(solution)/shard_map/pallas_call | solution.py:165
  31.2 1.6 %copy.6 = f32[64,512]{1,0:T(8,128)} copy(f32[64,512]{1,0:T(8,128)} %shard_map.46) | data formatting | bytes 262144

commit v2 on v1

--- a/solution.py
+++ b/solution.py
@@ -9,6 +9,8 @@
 
 BASE = 128
 CHUNKS = 4
+PIECES = 8
+JOIN = 4
 MESH = pl.DeviceIdType.MESH
 NN = (((1,), (0,)), ((), ()))
 NT = (((1,), (1,)), ((), ()))
@@ -25,10 +27,11 @@
     return dot(left[0], right[0]) + (dot(left[0], right[1]) + dot(left[1], right[0]))
 
 
-def kernel(n, diag_hbm, sub_hbm, right_hbm, bound_hbm, out_hbm,
+def kernel(n, group, diag_hbm, sub_hbm, right_hbm, bound_hbm, out_hbm,
            diag, sub, right, inverse, norm, inv_hi, inv_lo, subt_hi, subt_lo,
-           spike_hi, spike_lo, part, inflow, solved,
-           load_sem, send_sem, recv_sem, store_sem):
+           spike_hi, spike_lo, part, inflow, solved, spike, near_part, near_spike, joint,
+           load_sem, send_sem, skip_sem, recv_sem, store_sem, lead_send, lead_recv, part_sem,
+           core_send, core_recv, side_send, side_recv, relay_send, relay_recv):
     me = lax.axis_index("slab")
     width = diag.shape[0]
     columns = right.shape[0]
@@ -44,10 +47,23 @@
     def _():
         seed.start()
 
-    after, before = lax.rem(me + 1, n), lax.rem(me + n - 1, n)
+    paired = group == 4
+    seat = lax.axis_index("rhs")
+    twin, side = seat + 1 - 2 * lax.rem(seat, 2), seat + 2 - 4 * (seat // 2)
+    odd = lax.rem(me, 2) == 1
+    far = odd & (me >= JOIN)
+    giver = jnp.logical_not(odd) & (me >= JOIN) & (me < n - 1)
     barrier = pltpu.get_barrier_semaphore()
-    for other in (before, after):
-        pl.semaphore_signal(barrier, inc=1, device_id={"slab": other}, device_id_type=MESH)
+    greet = [(me >= 1, {"slab": me - 1}), (me < n - 1, {"slab": me + 1})]
+    if paired:
+        greet += [(odd & (me > JOIN), {"slab": me - 2}), (odd & (me >= JOIN - 1) & (me < n - 2), {"slab": me + 2})]
+        greet += [(far, {"rhs": twin}), (far, {"rhs": side})]
+
+    for there, target in greet:
+        @pl.when(there)
+        def _():
+            pl.semaphore_signal(barrier, inc=1, device_id=target, device_id_type=MESH)
+
 
     row = lax.broadcasted_iota(jnp.int32, (BASE, BASE), 0)
     col = lax.broadcasted_iota(jnp.int32, (BASE, BASE), 1)
@@ -97,40 +113,124 @@
     def take(pair, rows_at, cols_at):
         return pair[0][rows_at, cols_at], pair[1][rows_at, cols_at]
 
-    subt, inv, spike = (subt_hi, subt_lo), (inv_hi, inv_lo), (spike_hi, spike_lo)
+    subt, inv = (subt_hi, subt_lo), (inv_hi, inv_lo)
     top, bot, full = slice(0, cut), slice(cut, width), slice(0, width)
+
+    loads[2].wait()
+    given = split(right[...])
+    part[:, top] = mul((given[0][:, top], given[1][:, top]), take(inv, top, top), NT)
+    part[:, bot] = mul(given, take(inv, bot, full), NT)
+    pl.semaphore_wait(barrier, sum(jnp.where(there, 1, 0) for there, _ in greet))
+
+    def remote(src, dst, out_sem, in_sem, target):
+        return pltpu.make_async_remote_copy(
+            src_ref=src, dst_ref=dst, send_sem=out_sem, recv_sem=in_sem, device_id=target, device_id_type=MESH)
+
+    if paired:
+        share = width // group
+        step = share // PIECES
+
+        def strip(of, piece):
+            return pl.ds(pl.multiple_of(of * share + piece * step, step), step)
+
+        def lead_part():
+            return remote(part, near_part, part_sem.at[0], part_sem.at[1], {"slab": me + 1})
+
+        def lead(p):
+            return remote(spike.at[strip(seat, p)], near_spike.at[pl.ds(p * step, step)],
+                          lead_send.at[p], lead_recv.at[p], {"slab": me + 1})
+
+        def to_twin(p):
+            at = strip(seat, p)
+            return remote(joint.at[at], joint.at[at], core_send.at[p], core_recv.at[p], {"rhs": twin})
+
+        def to_side(p):
+            at = strip(seat, p)
+            return remote(joint.at[at], joint.at[at], side_send.at[p], side_recv.at[p], {"rhs": side})
+
+        def relay(p):
+            at = strip(side, p)
+            return remote(joint.at[at], joint.at[at], relay_send.at[p], relay_recv.at[p], {"rhs": twin})
 
     def put(rows_at, cols_at, value):
         high, low = split(value)
         spike_hi[rows_at, cols_at] = high
         spike_lo[rows_at, cols_at] = low
 
+    if paired:
+        @pl.when(giver)
+        def _():
+            own = pl.ds(pl.multiple_of(seat * share, share), share)
+            mine = subt_hi[own, :], subt_lo[own, :]
+            spike[own, :] = mul(mine, (inv_hi[...], inv_lo[...]), NT)
+            for p in range(PIECES):
+                lead(p).start()
+            lead_part().start()
+
     put(full, top, mul(take(subt, full, top), take(inv, top, top), NT))
     put(top, bot, mul(take(subt, top, top), take(inv, bot, top), NT))
     put(bot, bot, mul(take(subt, bot, full), take(inv, bot, full), NT))
-    loads[2].wait()
-    given = split(right[...])
-    part[:, top] = mul((given[0][:, top], given[1][:, top]), take(inv, top, top), NT)
-    part[:, bot] = mul(given, take(inv, bot, full), NT)
-
+
+    if paired:
+        @pl.when(giver)
+        def _():
+            for p in range(PIECES):
+                lead(p).wait_send()
+            lead_part().wait_send()
+
+        @pl.when(far)
+        def _():
+            whole = (spike_hi[...], spike_lo[...])
+            for p in range(PIECES):
+                lead(p).wait_recv()
+                joint[strip(seat, p), :] = -mul(split(near_spike[p * step:(p + 1) * step, :]), whole)
+                to_side(p).start()
+                to_twin(p).start()
+            for p in range(PIECES):
+                to_side(p).wait_recv()
+                relay(p).start()
+            lead_part().wait_recv()
+            part[...] = part[...] - mul(split(near_part[...]), whole)
+            for p in range(PIECES):
+                to_twin(p).wait_recv()
+            for p in range(PIECES):
+                relay(p).wait_recv()
+            high, low = split(joint[...])
+            spike_hi[...] = high
+            spike_lo[...] = low
+            for p in range(PIECES):
+                to_side(p).wait_send()
+                to_twin(p).wait_send()
+                relay(p).wait_send()
+
+    def rows_of(c):
+        return slice(c * rows, (c + 1) * rows)
 
     def send(c):
-        at = slice(c * rows, (c + 1) * rows)
-        return pltpu.make_async_remote_copy(
-            src_ref=solved.at[at], dst_ref=inflow.at[at], send_sem=send_sem.at[c], recv_sem=recv_sem.at[c],
-            device_id={"slab": after}, device_id_type=MESH)
+        at = rows_of(c)
+        return remote(solved.at[at], inflow.at[at], send_sem.at[c], recv_sem.at[c], {"slab": me + 1})
+
+    def skip(c):
+        at = rows_of(c)
+        return remote(solved.at[at], inflow.at[at], skip_sem.at[c], recv_sem.at[c], {"slab": me + 2})
 
     def store(c):
-        at = slice(c * rows, (c + 1) * rows)
+        at = rows_of(c)
         return pltpu.make_async_copy(solved.at[at], out_hbm.at[at], store_sem.at[c])
+
+    sends = jnp.logical_not(last)
+    skips = later = None
+    if paired:
+        sends = sends & (odd | (me < JOIN - 1))
+        skips = odd & (me >= JOIN - 1) & (me < n - 2)
+        later = skips & (me < n - 3)
 
     @pl.when(first)
     def _():
         seed.wait()
 
-    pl.semaphore_wait(barrier, 2)
     for c in range(CHUNKS):
-        at = slice(c * rows, (c + 1) * rows)
+        at = rows_of(c)
 
         @pl.when(jnp.logical_not(first))
         def _():
@@ -141,21 +241,37 @@
         both = dot(jnp.concatenate([high, low], axis=0), spike_hi[...])
         solved[at, :] = part[at, :] - (both[:rows] + both[rows:] + dot(high, spike_lo[...]))
 
-        @pl.when(jnp.logical_not(last))
+        @pl.when(sends & jnp.logical_not(later) if paired else sends)
         def _():
             send(c).start()
 
+        if paired:
+            @pl.when(skips)
+            def _():
+                skip(c).start()
+
         store(c).start()
+    if paired:
+        @pl.when(later)
+        def _():
+            for c in range(CHUNKS):
+                send(c).start()
+
     for c in range(CHUNKS):
         store(c).wait()
 
-        @pl.when(jnp.logical_not(last))
+        @pl.when(sends)
         def _():
             send(c).wait_send()
 
+        if paired:
+            @pl.when(skips)
+            def _():
+                skip(c).wait_send()
+
 
 def solution(mesh):
-    n = mesh.shape["slab"]
+    n, group = mesh.shape["slab"], mesh.shape["rhs"]
 
     def local(diag_blocks, sub_blocks, right_side, boundary):
         width = diag_blocks.shape[1]
@@ -163,7 +279,7 @@
         square, flat = (width, width), (columns, width)
         f32, bf16 = jnp.float32, jnp.bfloat16
         return pl.pallas_call(
-            functools.partial(kernel, n),
+            functools.partial(kernel, n, group),
             out_shape=jax.ShapeDtypeStruct(right_side.shape, f32),
             in_specs=[pl.BlockSpec(memory_space=pl.ANY)] * 4,
             out_specs=pl.BlockSpec(memory_space=pl.ANY),
@@ -172,8 +288,10 @@
                 pltpu.VMEM(square, f32), pltpu.VMEM(square, f32), pltpu.VMEM(square, bf16), pltpu.VMEM(square, bf16),
                 pltpu.VMEM(square, bf16), pltpu.VMEM(square, bf16), pltpu.VMEM(square, bf16), pltpu.VMEM(square, bf16),
                 pltpu.VMEM(flat, f32), pltpu.VMEM(flat, f32), pltpu.VMEM(flat, f32),
-                pltpu.SemaphoreType.DMA((4,)), pltpu.SemaphoreType.DMA((CHUNKS,)),
-                pltpu.SemaphoreType.DMA((CHUNKS,)), pltpu.SemaphoreType.DMA((CHUNKS,)),
+                pltpu.VMEM(square, f32), pltpu.VMEM(flat, f32), pltpu.VMEM((width // group, width), f32), pltpu.VMEM(square, f32),
+                pltpu.SemaphoreType.DMA((4,)), *[pltpu.SemaphoreType.DMA((CHUNKS,))] * 4,
+                *[pltpu.SemaphoreType.DMA((PIECES,))] * 2, pltpu.SemaphoreType.DMA((2,)),
+                *[pltpu.SemaphoreType.DMA((PIECES,))] * 6,
             ],
             compiler_params=pltpu.CompilerParams(collective_id=0, has_side_effects=True),
         )(diag_blocks, sub_blocks, right_side, boundary.T)

time: 32.9 us -> 29.7 us (0.903)
  the two profiles are of different devices: /device:TPU:30 before, /device:TPU:24 now
where the time goes in v2:
time: 29.7 us; the launch traced here: 29.5 us
  Pallas kernels  27.9 us (94%)
  local copies, waits for them, and re-layouts  1.57 us (5%)
    pallas_call x1, Pallas kernels, local(): pl.pallas_call(functools.partial(kernel, n, group), out_shape=jax.ShapeDt...  27.9 us
    unnamed x1, local copies, waits for them, and re-layouts  1.57 us

profile of v2, /device:TPU:24, one launch (start us, length us, event | category | flops | bytes accessed | tf_op | source)
XLA Modules:
  0.0 29.5 jit_solution(12314236097804066911)
XLA Ops:
  0.0 27.9 %shard_map.46 = f32[64,512]{1,0:T(8,128)} custom-call(f32[1,512,512]{2,1,0:T(8,128)} %diag_hbm.1, f32[1,512,512]{2,1,0:T(8,128)} %sub_hbm.1, f32[64,512]{1,0:T(8,128)} %right_hbm.1, f32[64,512]{1,0:T(8,128)} %bitcast.1), custom_call_target="tpu_custom_call" | custom-call | tf_op jit(solution)/shard_map/pallas_call | solution.py:281
  27.9 1.6 %copy.6 = f32[64,512]{1,0:T(8,128)} copy(f32[64,512]{1,0:T(8,128)} %shard_map.46) | data formatting | bytes 262144
